TPU v7x, 32 devices: a whole 2x2x4 slice. The times are simulated.
32 devices in a mesh: dp: 8 (over z, y), tensor: 4 (over x, core).
Axes of the slice: x: 2, y: 2, z: 4, core: 2. Of those that a mesh axis runs over, the one named last changes fastest.
Arguments:
- layer_input: bfloat16 [16384, 768], P(('dp', 'tensor')), may hold values from -6 to 6
- out_grad: bfloat16 [16384, 768], P(('dp', 'tensor')), may hold values from -6 to 6
- lengths: int32 [16], P('dp'), may hold values from 256 to 1024, as said below
- entry_weight: bfloat16 [768, 3, 768], P('dp', None, 'tensor'), may hold values from -0.21875 to 0.21875
- query_bias: float32 [768], replicated, may hold values from -3 to 3
- value_bias: float32 [768], replicated, may hold values from -3 to 3
- exit_weight: bfloat16 [768, 768], P('tensor', 'dp'), may hold values from -3.5 to 3.5
- exit_bias: float32 [768], replicated, may hold values from -2 to 2
- first_gain: float32 [768], replicated, may hold values from 0.5 to 1.5
- first_shift: float32 [768], replicated, may hold values from -1.5 to 1.5
- up_weight: bfloat16 [768, 3072], P('dp', 'tensor'), may hold values from -0.21875 to 0.21875
- up_bias: float32 [3072], replicated, may hold values from -3 to 3
- down_weight: bfloat16 [3072, 768], P('tensor', 'dp'), may hold values from -0.15625 to 0.15625
- down_bias: float32 [768], replicated, may hold values from -2 to 2
- second_gain: float32 [768], replicated, may hold values from 0.5 to 1.5
- second_shift: float32 [768], replicated, may hold values from -1.5 to 1.5
Outputs:
- layer_output: bfloat16 [16384, 768], P(('dp', 'tensor'))
- input_grad: float32 [16384, 768], P(('dp', 'tensor'))
- entry_grad: float32 [768, 3, 768], P('dp', None, 'tensor')
- query_bias_grad: float32 [768], replicated
- value_bias_grad: float32 [768], replicated
- exit_grad: float32 [768, 768], P('tensor', 'dp')
- exit_bias_grad: float32 [768], replicated
- first_gain_grad: float32 [768], replicated
- first_shift_grad: float32 [768], replicated
- up_grad: float32 [768, 3072], P('dp', 'tensor')
- up_bias_grad: float32 [3072], replicated
- down_grad: float32 [3072, 768], P('tensor', 'dp')
- down_bias_grad: float32 [768], replicated
- second_gain_grad: float32 [768], replicated
- second_shift_grad: float32 [768], replicated
Inputs may be any that keep to these rules, and one draw needn't show every extreme that they name: `lengths`: the number of leading tokens of each sequence that are not padding; some sequence is full and some has 256.
All inputs are finite; a program needn't handle non-finite values.
Results may differ from a plain program's by a relative error of at most 0.023.
Values may be sent and summed in bfloat16 or wider, within the bound.
A program may use at most 128 MiB of HBM per device.

v0:
```python
from functools import partial
import math
import jax
import jax.numpy as jnp
from jax import lax
from jax.sharding import PartitionSpec as P

HD = 64
LEN = 1024
EPSILON = 1e-12
NEG_FILL = -1e30


def layer_norm(rows, gain, shift):
    center = rows - jnp.mean(rows, axis=-1, keepdims=True)
    spread = jnp.mean(center * center, axis=-1, keepdims=True)
    return center * lax.rsqrt(spread + EPSILON) * gain + shift


def across(left, right):
    return lax.dot_general(
        left, right, (((0,), (0,)), ((), ())), preferred_element_type=jnp.float32
    )


def against(left, right):
    return lax.dot_general(
        left, right, (((1,), (1,)), ((), ())), preferred_element_type=jnp.float32
    )


def key_scores(queries, keys, length, scale):
    scores = jnp.einsum("qhd,khd->hqk", queries, keys, preferred_element_type=jnp.float32) * scale
    valid = jnp.arange(keys.shape[0]) < length
    return jnp.where(valid[None, None, :], scores, NEG_FILL)


def attend_sequence(item, scale, block):
    queries, keys, values, length = item
    blocks = queries.reshape(-1, block, queries.shape[1], queries.shape[2])

    def one_block(query_block):
        scores = key_scores(query_block, keys, length, scale)
        row_max = jnp.max(scores, axis=-1, keepdims=True)
        weights = jnp.exp(scores - row_max)
        total = jnp.sum(weights, axis=-1, keepdims=True)
        probs = (weights / total).astype(jnp.bfloat16)
        context = jnp.einsum("hqk,khd->qhd", probs, values, preferred_element_type=jnp.float32)
        return (context.astype(jnp.bfloat16), (row_max + jnp.log(total))[..., 0])

    return lax.map(one_block, blocks)


def attend_back(item, scale, block):
    queries, keys, values, length, context_grad, logsum = item
    heads = queries.shape[1]
    head_size = queries.shape[2]
    pieces = (
        queries.reshape(-1, block, heads, head_size),
        context_grad.reshape(-1, block, heads, head_size),
        logsum,
    )

    def one_block(carry, piece):
        key_total, value_total = carry
        query_block, grad_block, logsum_block = piece
        scores = key_scores(query_block, keys, length, scale)
        probs = jnp.exp(scores - logsum_block[..., None])
        value_total = value_total + jnp.einsum(
            "hqk,qhd->khd",
            probs.astype(jnp.bfloat16),
            grad_block,
            preferred_element_type=jnp.float32,
        )
        prob_grad = jnp.einsum(
            "qhd,khd->hqk", grad_block, values, preferred_element_type=jnp.float32
        )
        score_grad = (
            probs * (prob_grad - jnp.sum(probs * prob_grad, axis=-1, keepdims=True))
        ).astype(jnp.bfloat16)
        query_grad = (
            jnp.einsum("hqk,khd->qhd", score_grad, keys, preferred_element_type=jnp.float32) * scale
        )
        key_total = (
            key_total
            + jnp.einsum(
                "hqk,qhd->khd", score_grad, query_block, preferred_element_type=jnp.float32
            )
            * scale
        )
        return ((key_total, value_total), query_grad.astype(jnp.bfloat16))

    empty = jnp.zeros(keys.shape, jnp.float32)
    (key_total, value_total), query_grads = lax.scan(one_block, (empty, empty), pieces)
    return (
        query_grads.reshape(queries.shape),
        key_total.astype(jnp.bfloat16),
        value_total.astype(jnp.bfloat16),
    )


def place_slice(local, width, offset):
    return lax.dynamic_update_slice_in_dim(jnp.zeros((width,), jnp.float32), local, offset, 0)


def body(
    layer_input,
    out_grad,
    lengths,
    entry_weight,
    query_bias,
    value_bias,
    exit_weight,
    exit_bias,
    first_gain,
    first_shift,
    up_weight,
    up_bias,
    down_weight,
    down_bias,
    second_gain,
    second_shift,
):
    tensor_rank = lax.axis_index("tensor")
    own_rows = layer_input.shape[0]
    width = layer_input.shape[1]
    local_width = entry_weight.shape[2]
    local_hidden = up_weight.shape[1]
    full_hidden = up_bias.shape[0]
    head_count = local_width // HD
    seq_count = lengths.shape[0]
    group_rows = seq_count * LEN
    scale = 1.0 / math.sqrt(HD)
    block = min(512, LEN)
    entry_full, exit_full, up_full, down_full = (
        lax.all_gather(entry_weight, "dp", axis=0, tiled=True),
        lax.all_gather(exit_weight, "dp", axis=1, tiled=True),
        lax.all_gather(up_weight, "dp", axis=0, tiled=True),
        lax.all_gather(down_weight, "dp", axis=1, tiled=True),
    )
    entry_matrix = entry_full.reshape(width, 3 * local_width)
    query_local = lax.dynamic_slice_in_dim(query_bias, tensor_rank * local_width, local_width)
    value_local = lax.dynamic_slice_in_dim(value_bias, tensor_rank * local_width, local_width)
    up_local = lax.dynamic_slice_in_dim(up_bias, tensor_rank * local_hidden, local_hidden)
    rows_all = lax.all_gather(layer_input, "tensor", axis=0, tiled=True)
    offsets = jnp.stack([query_local, jnp.zeros_like(query_local), value_local])
    mixed = jnp.dot(rows_all, entry_matrix, preferred_element_type=jnp.float32).reshape(
        group_rows, 3, local_width
    )
    mixed = (mixed + offsets).astype(jnp.bfloat16)
    queries = mixed[:, 0].reshape(seq_count, LEN, head_count, HD)
    keys = mixed[:, 1].reshape(seq_count, LEN, head_count, HD)
    values = mixed[:, 2].reshape(seq_count, LEN, head_count, HD)
    context, logsum = lax.map(
        partial(attend_sequence, scale=scale, block=block), (queries, keys, values, lengths)
    )
    context = context.reshape(group_rows, local_width)
    attended = lax.psum_scatter(
        jnp.dot(context, exit_full, preferred_element_type=jnp.float32).astype(jnp.bfloat16),
        "tensor",
        scatter_dimension=0,
        tiled=True,
    ).astype(jnp.float32)
    first_sum = layer_input.astype(jnp.float32) + attended + exit_bias
    normed, first_pull = jax.vjp(layer_norm, first_sum, first_gain, first_shift)
    normed_low = normed.astype(jnp.bfloat16)
    normed_all = lax.all_gather(normed_low, "tensor", axis=0, tiled=True)
    upper = jnp.dot(normed_all, up_full, preferred_element_type=jnp.float32) + up_local
    active_full, gelu_pull = jax.vjp(partial(jax.nn.gelu, approximate=False), upper)
    active = active_full.astype(jnp.bfloat16)
    lowered = lax.psum_scatter(
        jnp.dot(
            lax.slice_in_dim(active, 0, lax.axis_size("tensor") * own_rows, axis=0),
            down_full,
            preferred_element_type=jnp.float32,
        ).astype(jnp.bfloat16),
        "tensor",
        scatter_dimension=0,
        tiled=True,
    ).astype(jnp.float32)
    second_sum = normed_low.astype(jnp.float32) + lowered + down_bias
    output, second_pull = jax.vjp(layer_norm, second_sum, second_gain, second_shift)
    layer_output = output.astype(jnp.bfloat16)
    entry_back, exit_back, up_back, down_back = (
        lax.all_gather(entry_weight, "dp", axis=0, tiled=True),
        lax.all_gather(exit_weight, "dp", axis=1, tiled=True),
        lax.all_gather(up_weight, "dp", axis=0, tiled=True),
        lax.all_gather(down_weight, "dp", axis=1, tiled=True),
    )
    entry_back_matrix = entry_back.reshape(width, 3 * local_width)
    second_grad, second_gain_grad, second_shift_grad = second_pull(out_grad.astype(jnp.float32))
    down_bias_grad = jnp.sum(second_grad, axis=0)
    lowered_all = lax.all_gather(second_grad.astype(jnp.bfloat16), "tensor", axis=0, tiled=True)
    down_grad_full = across(active, lowered_all)
    active_grad = against(lowered_all, down_back)
    upper_grad = gelu_pull(active_grad)[0].astype(jnp.bfloat16)
    up_bias_local = jnp.sum(upper_grad.astype(jnp.float32), axis=0)
    up_grad_full = across(normed_all, upper_grad)
    normed_back = lax.psum_scatter(
        against(upper_grad, up_back).astype(jnp.bfloat16), "tensor", scatter_dimension=0, tiled=True
    ).astype(jnp.float32)
    normed_grad = second_grad + normed_back
    first_grad, first_gain_grad, first_shift_grad = first_pull(normed_grad)
    exit_bias_grad = jnp.sum(first_grad, axis=0)
    attended_all = lax.all_gather(first_grad.astype(jnp.bfloat16), "tensor", axis=0, tiled=True)
    exit_grad_full = across(context, attended_all)
    context_grad = against(attended_all, exit_back).astype(jnp.bfloat16)
    query_grad, key_grad, value_grad = lax.map(
        partial(attend_back, scale=scale, block=block),
        (
            queries,
            keys,
            values,
            lengths,
            context_grad.reshape(seq_count, LEN, head_count, HD),
            logsum,
        ),
    )
    mixed_grad = jnp.stack(
        [
            query_grad.reshape(group_rows, local_width),
            key_grad.reshape(group_rows, local_width),
            value_grad.reshape(group_rows, local_width),
        ],
        axis=1,
    )
    query_bias_local = jnp.sum(mixed_grad[:, 0].astype(jnp.float32), axis=0)
    value_bias_local = jnp.sum(mixed_grad[:, 2].astype(jnp.float32), axis=0)
    mixed_flat = mixed_grad.reshape(group_rows, 3 * local_width)
    entry_grad_full = across(rows_all, mixed_flat).reshape(width, 3, local_width)
    input_back = lax.psum_scatter(
        against(mixed_flat, entry_back_matrix).astype(jnp.bfloat16),
        "tensor",
        scatter_dimension=0,
        tiled=True,
    ).astype(jnp.float32)
    input_grad = first_grad + input_back
    entry_grad, exit_grad, up_grad, down_grad = (
        lax.psum_scatter(entry_grad_full, "dp", scatter_dimension=0, tiled=True),
        lax.psum_scatter(exit_grad_full, "dp", scatter_dimension=1, tiled=True),
        lax.psum_scatter(up_grad_full, "dp", scatter_dimension=0, tiled=True),
        lax.psum_scatter(down_grad_full, "dp", scatter_dimension=1, tiled=True),
    )
    vectors = lax.psum(
        (
            place_slice(query_bias_local, width, tensor_rank * local_width),
            place_slice(value_bias_local, width, tensor_rank * local_width),
            exit_bias_grad,
            first_gain_grad,
            first_shift_grad,
            place_slice(up_bias_local, full_hidden, tensor_rank * local_hidden),
            down_bias_grad,
            second_gain_grad,
            second_shift_grad,
        ),
        ("dp", "tensor"),
    )
    return (
        layer_output,
        input_grad,
        entry_grad,
        vectors[0],
        vectors[1],
        exit_grad,
        vectors[2],
        vectors[3],
        vectors[4],
        up_grad,
        vectors[5],
        down_grad,
        vectors[6],
        vectors[7],
        vectors[8],
    )


def solution(mesh):
    return jax.shard_map(
        body,
        mesh=mesh,
        in_specs=(
            P(("dp", "tensor"), None),
            P(("dp", "tensor"), None),
            P("dp"),
            P("dp", None, "tensor"),
            P(),
            P(),
            P("tensor", "dp"),
            P(),
            P(),
            P(),
            P("dp", "tensor"),
            P(),
            P("tensor", "dp"),
            P(),
            P(),
            P(),
        ),
        out_specs=(
            P(("dp", "tensor"), None),
            P(("dp", "tensor"), None),
            P("dp", None, "tensor"),
            P(),
            P(),
            P("tensor", "dp"),
            P(),
            P(),
            P(),
            P("dp", "tensor"),
            P(),
            P("tensor", "dp"),
            P(),
            P(),
            P(),
        ),
        check_vma=False,
    )
```

profile of v0, /device:TPU:0, one launch (start us, length us, event | category | flops | bytes accessed | tf_op | source)
XLA Modules:
  0.0 812.9 jit_solution(9412491876366717269)
XLA Ops:
  11.2 35.4 %all_gather.29 = bf16[768,3,192]{2,0,1:T(8,128)(2,1)S(1)} all-gather(bf16[96,3,192]{2,0,1:T(8,128)(2,1)} %param.27), channel_id=1, replica_groups=mesh['dp'=8,'tensor'=4] {'dp'}, dimensions={0}, use_global_device_ids=true | all-gather | bytes 995328 | tf_op jit(solution)/shard_map/all_gather | solution.py:136
  47.4 33.0 %all_gather.30 = bf16[192,768]{0,1:T(8,128)(2,1)} all-gather(bf16[192,96]{0,1:T(8,128)(2,1)S(1)} %copy.73), channel_id=1, replica_groups=mesh['dp'=8,'tensor'=4] {'dp'}, dimensions={1}, use_global_device_ids=true | all-gather | bytes 331776 | tf_op jit(solution)/shard_map/all_gather | solution.py:137
  80.4 3.9 add_convert_fusion.1
  88.7 32.5 %while.54 = (s32[]{:T(128)}, bf16[2,2,512,3,64]{2,1,0,4,3:T(2,128)(2,1)}, f32[2,2,3,512]{3,2,1,0:T(4,128)}, bf16[2,1024,3,64]{1,3,2,0:T(8,128)(2,1)}, bf16[2,102...) while((s32[]{:T(128)}, ...), condition=%wide.region_5.6_spmd, body=%wide.region_0.5_spmd.sunk | while | flops 421625344 | bytes 24865084 | solution.py:154
  92.4 10.8 %while.57 = (s32[]{:T(128)}, bf16[2,512,3,64]{1,3,2,0:T(8,128)(2,1)S(1)}, f32[2,3,512]{2,1,0:T(4,128)S(1)}, s32[]{:T(128)}, bf16[2,512,3,64]{1,3,2,0:T(8,128)(2,...) while((s32[]{:T(128)}, bf16[2,512,3,64]{1,3,2,0:T(8,128)(2,1)S(1)}, ...), condition=%wide.region_4.4_spmd, body=%wide.region_1.3_spmd.sunk | while | flops 421625344 | bytes 20117612 | solution.py:51
  95.8 2.0 fusion.136
  101.2 2.0 fusion.136
  108.6 10.8 %while.57 = (s32[]{:T(128)}, bf16[2,512,3,64]{1,3,2,0:T(8,128)(2,1)S(1)}, f32[2,3,512]{2,1,0:T(4,128)S(1)}, s32[]{:T(128)}, bf16[2,512,3,64]{1,3,2,0:T(8,128)(2,...) while((s32[]{:T(128)}, bf16[2,512,3,64]{1,3,2,0:T(8,128)(2,1)S(1)}, ...), condition=%wide.region_4.4_spmd, body=%wide.region_1.3_spmd.sunk | while | flops 421625344 | bytes 20117612 | solution.py:51
  112.0 2.0 fusion.136
  117.4 2.0 fusion.136
  121.2 2.5 reshape.167
  123.8 2.7 convolution_convert_fusion.2
  127.4 37.9 %reduce-scatter.11.cloned.1.call-done = bf16[512,768]{1,0:T(8,128)(2,1)} async-done(((bf16[2048,768]{1,0:T(8,128)(2,1)}), bf16[512,768]{1,0:T(8,128)(2,1)}) %reduce-scatter.11.cloned.1.call-update) | async-done | bytes 786448 | tf_op jit(solution)/shard_map/reduce_scatter | solution.py:158
  171.4 28.8 %all-gather.9.cloned.1.call-done = bf16[2048,768]{1,0:T(8,128)(2,1)} async-done(((bf16[512,768]{1,0:T(8,128)(2,1)}), bf16[2048,768]{1,0:T(8,128)(2,1)}) %all-gather.9.cloned.1.call-update) | async-done | bytes 3145744 | tf_op jit(solution)/shard_map/all_gather | solution.py:167
  200.2 19.0 %multiply_convert_fusion.1 = (bf16[2048,768]{1,0:T(8,128)(2,1)}, f32[2048,768]{1,0:T(8,128)}, f32[2048,768]{1,0:T(8,128)}) fusion(f32[768]{0:T(1024)S(1)} %dynamic_slice.58, bf16[2048,768]{1,0:T(8,128)(2,1)} %all-gather.9.cloned.1.call-done, bf16[768,768]{1,0:T(8,128)(2,1)} %all-gather.11.cloned.1.call-done), kind=kOutput, calls=%fused_computation.68 | convolution fusion | flops 2519728128 | bytes 20057088 | tf_op jit(solution)/shard_map/dot_general | solution.py:168
  219.1 24.5 %all-gather.13.cloned.1.call-done = bf16[768,768]{0,1:T(8,128)(2,1)} async-done(((bf16[768,96]{0,1:T(8,128)(2,1)}), bf16[768,768]{0,1:T(8,128)(2,1)}) %all-gather.13.cloned.1.call-update) | async-done | bytes 1179664 | tf_op jit(solution)/shard_map/all_gather | solution.py:139
  243.7 6.5 convolution_convert_fusion.1
  250.3 36.1 %reduce-scatter.13.cloned.1.call-done = bf16[512,768]{1,0:T(8,128)(2,1)} async-done(((bf16[2048,768]{1,0:T(8,128)(2,1)}), bf16[512,768]{1,0:T(8,128)(2,1)}) %reduce-scatter.13.cloned.1.call-update) | async-done | bytes 786448 | tf_op jit(solution)/shard_map/reduce_scatter | solution.py:171
  295.4 28.2 %all-gather.15.cloned.1.call-done = bf16[2048,768]{1,0:T(8,128)(2,1)} async-done(((bf16[512,768]{1,0:T(8,128)(2,1)}), bf16[2048,768]{1,0:T(8,128)(2,1)}) %all-gather.15.cloned.1.call-update) | async-done | bytes 3145744 | tf_op jit(solution)/shard_map/all_gather | solution.py:193
  323.6 11.1 %convert_reduce_fusion = (f32[768]{0:T(1024)}, bf16[2048,768]{1,0:T(8,128)(2,1)S(1)}) fusion(f32[2048,768]{1,0:T(8,128)} %get-tuple-element.413, f32[2048,768]{1,0:T(8,128)} %get-tuple-element.428, f32[768]{0:T(1024)S(1)} %copy-done.40, bf16[2048,768]{1,0:T(8,128)(2,1)} %all-gather.15.cloned.1.call-done, bf16[768,768]{0,1:T(8,128)(2,1)} %all-gather.13.cloned.1.call-done), kind=kOutput, calls=%fused_computation.66 | convolution fusion | flops 2442657024 | bytes 20060160 | tf_op jit(solution)/shard_map/dot_general | solution.py:27
  336.4 4.1 convolution_convert_fusion
  340.6 37.8 %reduce-scatter.15.cloned.1.call-done = bf16[512,768]{1,0:T(8,128)(2,1)} async-done(((bf16[2048,768]{1,0:T(8,128)(2,1)}), bf16[512,768]{1,0:T(8,128)(2,1)}) %reduce-scatter.15.cloned.1.call-update) | async-done | bytes 786448 | tf_op jit(solution)/shard_map/reduce_scatter | solution.py:199
  378.4 3.1 multiply_reduce_fusion.1
  387.0 28.4 %all-gather.17.cloned.1.call-done = bf16[2048,768]{1,0:T(8,128)(2,1)} async-done(((bf16[512,768]{1,0:T(8,128)(2,1)}), bf16[2048,768]{1,0:T(8,128)(2,1)}) %all-gather.17.cloned.1.call-update) | async-done | bytes 3145744 | tf_op jit(solution)/shard_map/all_gather | solution.py:205
  415.5 3.1 convolution_convert_fusion.3
  420.2 57.5 %while.56 = (s32[]{:T(128)}, bf16[2,1024,3,64]{3,2,1,0:T(4,128)(2,1)}, bf16[2,1024,3,64]{1,3,2,0:T(8,128)(2,1)}, bf16[2,1024,3,64]{1,3,2,0:T(8,128)(2,1)}, bf16[...) while((s32[]{:T(128)}, ...), condition=%wide.region_21.22_spmd, body=%wide.region_17.21_spmd.sunk | while | flops 1031798272 | bytes 74459688 | solution.py:208
  426.0 18.2 %while.58 = (s32[]{:T(128)}, f32[1024,3,64]{0,2,1:T(8,128)S(1)}, f32[1024,3,64]{0,2,1:T(8,128)}, bf16[2,512,3,64]{1,3,2,0:T(8,128)(2,1)S(1)}, bf16[2,512,3,64]{1...) while((s32[]{:T(128)}, f32[1024,3,64]{0,2,1:T(8,128)S(1)}, ...), condition=%wide.region_20.20_spmd.clone, body=%wide.region_18.19_spmd.clone.sunk | while | flops 1031405056 | bytes 58837208 | solution.py:94
  429.4 2.1 multiply_reduce_fusion.6
  438.5 2.1 multiply_reduce_fusion.6
  454.7 18.2 %while.58 = (s32[]{:T(128)}, f32[1024,3,64]{0,2,1:T(8,128)S(1)}, f32[1024,3,64]{0,2,1:T(8,128)}, bf16[2,512,3,64]{1,3,2,0:T(8,128)(2,1)S(1)}, bf16[2,512,3,64]{1...) while((s32[]{:T(128)}, f32[1024,3,64]{0,2,1:T(8,128)S(1)}, ...), condition=%wide.region_20.20_spmd.clone, body=%wide.region_18.19_spmd.clone.sunk | while | flops 1031405056 | bytes 58837208 | solution.py:94
  458.2 2.1 multiply_reduce_fusion.6
  467.3 2.1 multiply_reduce_fusion.6
  477.7 4.5 convolution_bitcast_fusion
  482.5 3.6 copy.80
  486.1 2.6 stack_reshape.9
  493.9 2.5 stack_reshape.11
  498.4 6.1 bitcast_convert_fusion
  504.5 7.0 fusion.70
  511.9 7.0 fusion.71
  518.9 4.6 fusion.69
  523.6 2.0 copy.83
  526.2 3.8 convert_reduce_fusion.1
  530.5 40.9 %all-reduce = (f32[768]{0:T(1024)}, f32[768]{0:T(1024)}, f32[768]{0:T(1024)}, f32[768]{0:T(1024)}, f32[768]{0:T(1024)}, /*index=5*/f32[3072]{0:T(1024)}, f32[768]{0:T(1024)}, f32[768]{0:T(1024)}, f32[768]{0:T(1024)}) all-reduce(f32[768]{0:T(1024)S(1)} %dynamic_update_slice.38, ...), channel_id=1, replica_groups=mesh['dp'=8,'tensor'=4] {'dp','tensor'}, use_global_device_ids=true, to_apply=%region_25.26 | all-reduce | flops 9216 | bytes 73728 | tf_op jit(solution)/shard_map/psum | solution.py:244
  573.0 12.3 %reduce-scatter.17.cloned.1.call-done = bf16[512,768]{1,0:T(8,128)(2,1)} async-done(((bf16[2048,768]{1,0:T(8,128)(2,1)}), bf16[512,768]{1,0:T(8,128)(2,1)}) %reduce-scatter.17.cloned.1.call-update) | async-done | bytes 786448 | tf_op jit(solution)/shard_map/reduce_scatter | solution.py:231
  585.3 2.5 convert_add_fusion
  587.8 71.2 %reduce-scatter.21.cloned.1.call-done = f32[96,768]{1,0:T(8,128)} async-done(((f32[768,768]{1,0:T(8,128)}), f32[96,768]{1,0:T(8,128)}) %reduce-scatter.21.cloned.1.call-update) | async-done | bytes 294928 | tf_op jit(solution)/shard_map/reduce_scatter | solution.py:241
  659.1 72.9 %reduce-scatter.23.cloned.1.call-done = f32[768,96]{0,1:T(8,128)} async-done(((f32[768,768]{0,1:T(8,128)}), f32[768,96]{0,1:T(8,128)}) %reduce-scatter.23.cloned.1.call-update) | async-done | bytes 294928 | tf_op jit(solution)/shard_map/reduce_scatter | solution.py:242
  732.0 73.3 %reduce-scatter.19.cloned.1.call-done = f32[96,3,192]{2,0,1:T(8,128)} async-done(((f32[768,3,192]{2,0,1:T(8,128)}), f32[96,3,192]{2,0,1:T(8,128)}) %reduce-scatter.19.cloned.1.call-update) | async-done | bytes 221200 | tf_op jit(solution)/shard_map/reduce_scatter | solution.py:239
  (284 shorter events, 116.7 us)
Async XLA Ops:
  8.0 72.4 %all-gather.7.cloned.1.call-start = ((), (), s32[]{:S(2)}) async-start(), calls=%async_computation.8 | async-start | bytes 3932160 | tf_op jit(solution)/shard_map/all_gather | solution.py:145
  8.7 156.6 %reduce-scatter.11.cloned.1.call-start = ((), (), s32[]{:S(2)}) async-start(), calls=%async_computation.9 | async-start | bytes 3932160 | tf_op jit(solution)/shard_map/reduce_scatter | solution.py:158
  46.6 37.7 %copy-start.14 = (bf16[768,3,192]{2,0,1:T(8,128)(2,1)}, bf16[768,3,192]{2,0,1:T(8,128)(2,1)S(1)}, u32[]{:S(2)}) copy-start(bf16[768,3,192]{2,0,1:T(8,128)(2,1)S(1)} %all_gather.29) | copy-start | bytes 2654212
  88.7 35.1 %copy-start.16 = (bf16[192,768]{0,1:T(8,128)(2,1)S(1)}, bf16[192,768]{0,1:T(8,128)(2,1)}, u32[]{:S(2)}) copy-start(bf16[192,768]{0,1:T(8,128)(2,1)} %all_gather.30) | copy-start | bytes 884740
  123.7 41.6 %copy-start = (bf16[512,768]{1,0:T(8,128)(2,1)S(1)}, bf16[512,768]{1,0:T(8,128)(2,1)}, u32[]{:S(2)}) copy-start(bf16[512,768]{1,0:T(8,128)(2,1)} %param.24) | copy-start | bytes 2359300
  123.8 41.6 %copy-start.21 = (f32[768]{0:T(1024)S(1)}, f32[768]{0:T(1024)}, u32[]{:S(2)}) copy-start(f32[768]{0:T(1024)} %param.31) | copy-start | bytes 9220
  126.5 42.0 %copy-start.23 = (f32[768]{0:T(1024)S(1)}, f32[768]{0:T(1024)}, u32[]{:S(2)}) copy-start(f32[768]{0:T(1024)} %param.32) | copy-start | bytes 9220
  126.5 42.0 %copy-start.37 = (f32[768]{0:T(1024)S(1)}, f32[768]{0:T(1024)}, u32[]{:S(2)}) copy-start(f32[768]{0:T(1024)} %param.33) | copy-start | bytes 9220
  126.5 44.9 %all-gather.11.cloned.1.call-start = ((), (), s32[]{:S(2)}) async-start(), calls=%async_computation.11 | async-start | bytes 1327104 | tf_op jit(solution)/shard_map/all_gather | solution.py:138
  127.1 73.1 %all-gather.9.cloned.1.call-start = ((), (), s32[]{:S(2)}) async-start(), calls=%async_computation.10 | async-start | bytes 3932160 | tf_op jit(solution)/shard_map/all_gather | solution.py:167
  168.4 50.7 %copy-start.29 = (f32[512]{0:T(512)}, f32[512]{0:T(512)S(1)}, u32[]{:S(2)}) copy-start(f32[512]{0:T(512)S(1)} %multiply_reduce_fusion.4) | copy-start | bytes 6148
  168.5 50.6 %copy-start.24 = (f32[512]{0:T(512)}, f32[512]{0:T(512)S(1)}, u32[]{:S(2)}) copy-start(f32[512]{0:T(512)S(1)} %fusion.62) | copy-start | bytes 6148
  169.9 73.8 %all-gather.13.cloned.1.call-start = ((), (), s32[]{:S(2)}) async-start(), calls=%async_computation.12 | async-start | bytes 1327104 | tf_op jit(solution)/shard_map/all_gather | solution.py:139
  170.5 116.0 %reduce-scatter.13.cloned.1.call-start = ((), (), s32[]{:S(2)}) async-start(), calls=%async_computation.13 | async-start | bytes 3932160 | tf_op jit(solution)/shard_map/reduce_scatter | solution.py:171
  171.3 47.8 %copy-start.39 = (f32[768]{0:T(1024)}, f32[768]{0:T(1024)S(1)}, u32[]{:S(2)}) copy-start(f32[768]{0:T(1024)S(1)} %dynamic_slice.58) | copy-start | bytes 9220
  250.2 36.2 %copy-start.1 = (bf16[512,768]{1,0:T(8,128)(2,1)S(1)}, bf16[512,768]{1,0:T(8,128)(2,1)}, u32[]{:S(2)}) copy-start(bf16[512,768]{1,0:T(8,128)(2,1)} %add_convert_fusion.3) | copy-start | bytes 2359300
  250.2 36.2 %copy-start.22 = (f32[768]{0:T(1024)S(1)}, f32[768]{0:T(1024)}, u32[]{:S(2)}) copy-start(f32[768]{0:T(1024)} %param.37) | copy-start | bytes 9220
  250.2 39.4 %copy-start.20 = (bf16[512,768]{1,0:T(8,128)(2,1)S(1)}, bf16[512,768]{1,0:T(8,128)(2,1)}, u32[]{:S(2)}) copy-start(bf16[512,768]{1,0:T(8,128)(2,1)} %param.25) | copy-start | bytes 2359300
  250.2 73.4 %all-gather.15.cloned.1.call-start = ((), (), s32[]{:S(2)}) async-start(), calls=%async_computation.14 | async-start | bytes 3932160 | tf_op jit(solution)/shard_map/all_gather | solution.py:193
  286.4 3.2 copy-start.36
  286.4 4.6 copy-start.41
  292.8 30.9 %copy-start.40 = (f32[768]{0:T(1024)S(1)}, f32[768]{0:T(1024)}, u32[]{:S(2)}) copy-start(f32[768]{0:T(1024)} %copy-done.39) | copy-start | bytes 9220
  292.8 42.0 %copy-start.26 = (f32[512]{0:T(512)}, f32[512]{0:T(512)S(1)}, u32[]{:S(2)}) copy-start(f32[512]{0:T(512)S(1)} %negate_multiply_fusion.2) | copy-start | bytes 6148
  295.0 83.4 %reduce-scatter.15.cloned.1.call-start = ((), (), s32[]{:S(2)}) async-start(), calls=%async_computation.15 | async-start | bytes 3932160 | tf_op jit(solution)/shard_map/reduce_scatter | solution.py:199
  323.6 12.8 %copy-start.42 = (bf16[768,768]{1,0:T(8,128)(2,1)S(1)}, bf16[768,768]{1,0:T(8,128)(2,1)}, u32[]{:S(2)}) copy-start(bf16[768,768]{1,0:T(8,128)(2,1)} %all-gather.11.cloned.1.call-done) | copy-start | bytes 3538948
  340.5 37.9 %copy-start.3 = (f32[512,768]{1,0:T(8,128)S(1)}, f32[512,768]{1,0:T(8,128)}, u32[]{:S(2)}) copy-start(f32[512,768]{1,0:T(8,128)} %copy-done.2) | copy-start | bytes 4718596
  340.5 37.9 %copy-start.25 = (f32[512]{0:T(512)S(1)}, f32[512]{0:T(512)}, u32[]{:S(2)}) copy-start(f32[512]{0:T(512)} %copy-done.24) | copy-start | bytes 6148
  340.5 74.9 %all-gather.17.cloned.1.call-start = ((), (), s32[]{:S(2)}) async-start(), calls=%async_computation.16 | async-start | bytes 3932160 | tf_op jit(solution)/shard_map/all_gather | solution.py:205
  378.4 3.8 copy-start.8
  378.4 3.8 copy-start.17
  386.8 184.6 %reduce-scatter.25.cloned.1.call-start = ((), (), s32[]{:S(2)}) async-start(), calls=%async_computation.21 | async-start | bytes 884736
  444.2 3.8 copy-start.6
  473.0 3.7 copy-start.6
  477.7 4.8 copy-start.13
  482.2 103.1 %reduce-scatter.17.cloned.1.call-start = ((), (), s32[]{:S(2)}) async-start(), calls=%async_computation.17 | async-start | bytes 3932160 | tf_op jit(solution)/shard_map/reduce_scatter | solution.py:231
  486.1 6.2 copy-start.18
  492.3 6.1 copy-start.15
  504.5 154.6 %reduce-scatter.21.cloned.1.call-start = ((), (), s32[]{:S(2)}) async-start(), calls=%async_computation.19 | async-start | bytes 2654208 | tf_op jit(solution)/shard_map/reduce_scatter | solution.py:241
  511.6 220.4 %reduce-scatter.23.cloned.1.call-start = ((), (), s32[]{:S(2)}) async-start(), calls=%async_computation.20 | async-start | bytes 2654208 | tf_op jit(solution)/shard_map/reduce_scatter | solution.py:242
  518.9 286.4 %reduce-scatter.19.cloned.1.call-start = ((), (), s32[]{:S(2)}) async-start(), calls=%async_computation.18 | async-start | bytes 2654208 | tf_op jit(solution)/shard_map/reduce_scatter | solution.py:239
  525.5 4.9 copy-start.30
  525.5 4.9 copy-start.31
  525.5 4.9 copy-start.32
  525.5 4.9 copy-start.33
  525.5 4.9 copy-start.34
  525.5 4.9 copy-start.35
  525.5 59.8 %copy-start.10 = (f32[512,768]{1,0:T(8,128)S(1)}, f32[512,768]{1,0:T(8,128)}, u32[]{:S(2)}) copy-start(f32[512,768]{1,0:T(8,128)} %copy-done.9) | copy-start | bytes 4718596
  525.6 59.8 %copy-start.28 = (f32[512]{0:T(512)S(1)}, f32[512]{0:T(512)}, u32[]{:S(2)}) copy-start(f32[512]{0:T(512)} %copy-done.27) | copy-start | bytes 6148
  (18 other events, 32.4 us)
Sparse Core Ops, SparseCore 0:
  10.4 31.2 all-gather.6
  126.6 38.6 reduce-scatter.10
  295.1 28.5 all-gather.14
  386.9 28.4 all-gather.16
Sparse Core Ops, SparseCore 1:
  129.2 42.1 all-gather.10
  173.4 26.7 all-gather.8
  202.2 41.4 all-gather.12
  250.3 36.1 reduce-scatter.12
  340.6 37.7 reduce-scatter.14
  482.3 63.3 reduce-scatter.24
  548.0 37.2 reduce-scatter.16
  589.3 69.7 reduce-scatter.20
  663.0 68.9 reduce-scatter.22
  736.1 69.2 reduce-scatter.18
where the time goes:
time: 823 us; the launch traced here: 813 us
  waiting for transfers between devices  454 us (55%)
  matrix products  118 us (14%)
  blocking collectives  109 us (13%)
  local copies, waits for them, and re-layouts  66.9 us (8%)
  other arithmetic  46.2 us (6%)
  between operations  16.3 us (2%)
    reduce_scatter x1, waiting for transfers between devices, body(): lax.psum_scatter(entry_grad_full, 'dp', scatter_dimension=0, tiled=True)  73.3 us
    reduce_scatter x1, waiting for transfers between devices, body(): lax.psum_scatter(down_grad_full, 'dp', scatter_dimension=1, tiled=True)  72.9 us
    reduce_scatter x1, waiting for transfers between devices, body(): lax.psum_scatter(up_grad_full, 'dp', scatter_dimension=0, tiled=True)  71.2 us
    psum x1, blocking collectives, body(): lax.psum((place_slice(query_bias_local, width, tensor_rank * local_width)...  40.9 us
    reduce_scatter x1, waiting for transfers between devices, body(): lax.psum_scatter(jnp.dot(context, exit_full, preferred_element_type=jnp.f...  37.9 us
    reduce_scatter x1, waiting for transfers between devices, body(): lax.psum_scatter(against(upper_grad, up_back).astype(jnp.bfloat16), 'tens...  37.8 us
    reduce_scatter x1, waiting for transfers between devices, body(): lax.psum_scatter(jnp.dot(lax.slice_in_dim(active, 0, lax.axis_size('tenso...  36.1 us
    all_gather x1, blocking collectives, body(): lax.all_gather(entry_weight, 'dp', axis=0, tiled=True)  35.4 us
  transfers between devices with their start and end apart: 14, of which 12 were waited for; matrix products, arithmetic and copies ran while one was open for 10% of the time, Pallas kernels for 0%

commit v1 on v0

--- a/solution.py
+++ b/solution.py
@@ -9,6 +9,18 @@
 LEN = 1024
 EPSILON = 1e-12
 NEG_FILL = -1e30
+
+
+def doubled_up(value, axis, dim):
+    ways, here, step = (lax.axis_size(axis), lax.axis_index(axis), value.shape[dim])
+    line, have = (value, 1)
+    while have < ways:
+        line = jnp.concatenate(
+            [line, lax.ppermute(line, axis, [(d, (d - have) % ways) for d in range(ways)])],
+            axis=dim,
+        )
+        have = 2 * have
+    return jnp.roll(line, here * step, axis=dim)
 
 
 def layer_norm(rows, gain, shift):
@@ -136,7 +148,7 @@
         lax.all_gather(entry_weight, "dp", axis=0, tiled=True),
         lax.all_gather(exit_weight, "dp", axis=1, tiled=True),
         lax.all_gather(up_weight, "dp", axis=0, tiled=True),
-        lax.all_gather(down_weight, "dp", axis=1, tiled=True),
+        doubled_up(down_weight, "dp", 1),
     )
     entry_matrix = entry_full.reshape(width, 3 * local_width)
     query_local = lax.dynamic_slice_in_dim(query_bias, tensor_rank * local_width, local_width)

time: 823 us -> 853 us (1.036)
  waiting for transfers between devices: 454 us -> 470 us
    ppermute x0 -> x3, waiting for transfers between devices: none -> 32.6 us  [doubled_up(): lax.ppermute(line, axis, [(d, (d - have) % ways) for d in range(ways)])]
    all_gather x1, waiting for transfers between devices: 28.8 us -> 0.01 us  [body(): normed_all = lax.all_gather(normed_low, 'tensor', axis=0, tiled=True)]
    all_gather x1, waiting for transfers between devices: 24.5 us -> 34.7 us  [body(): lax.all_gather(down_weight, 'dp', axis=1, tiled=True)]
  transfers between devices with their start and end apart: 14 -> 17, of which waited for: 12 -> 13; matrix products, arithmetic and copies ran while one was open for 10% -> 9% of each run, Pallas kernels for 0% -> 0%
where the time goes in v1:
time: 853 us; the launch traced here: 843 us
  waiting for transfers between devices  470 us (55%)
  matrix products  117 us (14%)
  blocking collectives  109 us (13%)
  local copies, waits for them, and re-layouts  74.6 us (9%)
  other arithmetic  47.1 us (6%)
  between operations  16.3 us (2%)
    reduce_scatter x1, waiting for transfers between devices, body(): lax.psum_scatter(down_grad_full, 'dp', scatter_dimension=1, tiled=True)  73.2 us
    reduce_scatter x1, waiting for transfers between devices, body(): lax.psum_scatter(entry_grad_full, 'dp', scatter_dimension=0, tiled=True)  73.1 us
    reduce_scatter x1, waiting for transfers between devices, body(): lax.psum_scatter(up_grad_full, 'dp', scatter_dimension=0, tiled=True)  71.2 us
    psum x1, blocking collectives, body(): lax.psum((place_slice(query_bias_local, width, tensor_rank * local_width)...  40.9 us
    reduce_scatter x1, waiting for transfers between devices, body(): lax.psum_scatter(against(upper_grad, up_back).astype(jnp.bfloat16), 'tens...  38 us
    reduce_scatter x1, waiting for transfers between devices, body(): lax.psum_scatter(jnp.dot(lax.slice_in_dim(active, 0, lax.axis_size('tenso...  38 us
    reduce_scatter x1, waiting for transfers between devices, body(): lax.psum_scatter(jnp.dot(context, exit_full, preferred_element_type=jnp.f...  38 us
    all_gather x1, blocking collectives, body(): lax.all_gather(entry_weight, 'dp', axis=0, tiled=True)  35.4 us
  transfers between devices with their start and end apart: 17, of which 13 were waited for; matrix products, arithmetic and copies ran while one was open for 9% of the time, Pallas kernels for 0%

profile of v1, /device:TPU:0, one launch (start us, length us, event | category | flops | bytes accessed | tf_op | source)
XLA Modules:
  0.0 842.8 jit_solution(3630657457750057699)
XLA Ops:
  11.2 35.4 %all_gather.28 = bf16[768,3,192]{2,0,1:T(8,128)(2,1)S(1)} all-gather(bf16[96,3,192]{2,0,1:T(8,128)(2,1)} %param.27), channel_id=1, replica_groups=mesh['dp'=8,'tensor'=4] {'dp'}, dimensions={0}, use_global_device_ids=true | all-gather | bytes 995328 | tf_op jit(solution)/shard_map/all_gather | solution.py:148
  47.4 33.0 %all_gather.29 = bf16[192,768]{0,1:T(8,128)(2,1)} all-gather(bf16[192,96]{0,1:T(8,128)(2,1)S(1)} %copy.73), channel_id=1, replica_groups=mesh['dp'=8,'tensor'=4] {'dp'}, dimensions={1}, use_global_device_ids=true | all-gather | bytes 331776 | tf_op jit(solution)/shard_map/all_gather | solution.py:149
  80.4 3.9 add_convert_fusion.1
  88.7 32.5 %while.54 = (s32[]{:T(128)}, bf16[2,2,512,3,64]{2,1,0,4,3:T(2,128)(2,1)}, f32[2,2,3,512]{3,2,1,0:T(4,128)}, bf16[2,1024,3,64]{1,3,2,0:T(8,128)(2,1)}, bf16[2,102...) while((s32[]{:T(128)}, ...), condition=%wide.region_5.6_spmd, body=%wide.region_0.5_spmd.sunk | while | flops 421625344 | bytes 24865084 | solution.py:166
  92.4 10.8 %while.57 = (s32[]{:T(128)}, bf16[2,512,3,64]{1,3,2,0:T(8,128)(2,1)S(1)}, f32[2,3,512]{2,1,0:T(4,128)S(1)}, s32[]{:T(128)}, bf16[2,512,3,64]{1,3,2,0:T(8,128)(2,...) while((s32[]{:T(128)}, bf16[2,512,3,64]{1,3,2,0:T(8,128)(2,1)S(1)}, ...), condition=%wide.region_4.4_spmd, body=%wide.region_1.3_spmd.sunk | while | flops 421625344 | bytes 20117612 | solution.py:63
  95.8 2.0 fusion.137
  108.6 10.8 %while.57 = (s32[]{:T(128)}, bf16[2,512,3,64]{1,3,2,0:T(8,128)(2,1)S(1)}, f32[2,3,512]{2,1,0:T(4,128)S(1)}, s32[]{:T(128)}, bf16[2,512,3,64]{1,3,2,0:T(8,128)(2,...) while((s32[]{:T(128)}, bf16[2,512,3,64]{1,3,2,0:T(8,128)(2,1)S(1)}, ...), condition=%wide.region_4.4_spmd, body=%wide.region_1.3_spmd.sunk | while | flops 421625344 | bytes 20117612 | solution.py:63
  121.2 2.5 reshape.167
  123.8 2.7 convolution_convert_fusion.2
  127.4 38.0 %reduce-scatter.11.cloned.1.call-done = bf16[512,768]{1,0:T(8,128)(2,1)} async-done(((bf16[2048,768]{1,0:T(8,128)(2,1)}), bf16[512,768]{1,0:T(8,128)(2,1)}) %reduce-scatter.11.cloned.1.call-update) | async-done | bytes 786448 | tf_op jit(solution)/shard_map/reduce_scatter | solution.py:170
  170.0 4.3 collective-permute-start
  174.3 3.0 collective-permute-done
  178.9 6.2 collective-permute-done.1
  189.4 23.5 %collective-permute-done.2 = bf16[768,384]{0,1:T(8,128)(2,1)S(1)} collective-permute-done((bf16[768,384]{0,1:T(8,128)(2,1)}, bf16[768,384]{0,1:T(8,128)(2,1)S(1)}, u32[]{:S(2)}, u32[]{:S(2)}) %collective-permute-start.2) | collective-permute-done | bytes 589856 | tf_op jit(solution)/shard_map/ppermute | solution.py:19
  216.7 18.7 %multiply_convert_fusion.1 = (bf16[2048,768]{1,0:T(8,128)(2,1)S(1)}, f32[2048,768]{1,0:T(8,128)}, f32[2048,768]{1,0:T(8,128)}) fusion(f32[768]{0:T(1024)S(1)} %dynamic_slice.62, bf16[2048,768]{1,0:T(8,128)(2,1)} %all-gather.9.cloned.1.call-done, bf16[768,768]{1,0:T(8,128)(2,1)} %all-gather.11.cloned.1.call-done), kind=kOutput, calls=%fused_computation.68 | convolution fusion | flops 2519728128 | bytes 20057088 | tf_op jit(solution)/shard_map/dot_general | solution.py:180
  237.1 5.4 convolution_convert_fusion.1
  243.3 38.0 %reduce-scatter.13.cloned.1.call-done = bf16[512,768]{1,0:T(8,128)(2,1)} async-done(((bf16[2048,768]{1,0:T(8,128)(2,1)}), bf16[512,768]{1,0:T(8,128)(2,1)}) %reduce-scatter.13.cloned.1.call-update) | async-done | bytes 786448 | tf_op jit(solution)/shard_map/reduce_scatter | solution.py:183
  290.3 34.7 %all-gather.15.cloned.1.call-done = bf16[768,768]{0,1:T(8,128)(2,1)} async-done(((bf16[768,96]{0,1:T(8,128)(2,1)}), bf16[768,768]{0,1:T(8,128)(2,1)}) %all-gather.15.cloned.1.call-update) | async-done | bytes 1179664 | tf_op jit(solution)/shard_map/all_gather | solution.py:200
  324.9 28.3 %all-gather.13.cloned.1.call-done = bf16[2048,768]{1,0:T(8,128)(2,1)} async-done(((bf16[512,768]{1,0:T(8,128)(2,1)}), bf16[2048,768]{1,0:T(8,128)(2,1)}) %all-gather.13.cloned.1.call-update) | async-done | bytes 3145744 | tf_op jit(solution)/shard_map/all_gather | solution.py:205
  353.3 11.1 %convert_reduce_fusion = (f32[768]{0:T(1024)}, bf16[2048,768]{1,0:T(8,128)(2,1)S(1)}) fusion(f32[2048,768]{1,0:T(8,128)} %get-tuple-element.413, f32[2048,768]{1,0:T(8,128)} %get-tuple-element.428, f32[768]{0:T(1024)S(1)} %copy-done.41, bf16[2048,768]{1,0:T(8,128)(2,1)} %all-gather.13.cloned.1.call-done, bf16[768,768]{0,1:T(8,128)(2,1)} %all-gather.15.cloned.1.call-done), kind=kOutput, calls=%fused_computation.66 | convolution fusion | flops 2442657024 | bytes 20060160 | tf_op jit(solution)/shard_map/dot_general | solution.py:39
  366.1 4.1 convolution_convert_fusion
  370.2 38.0 %reduce-scatter.15.cloned.1.call-done = bf16[512,768]{1,0:T(8,128)(2,1)} async-done(((bf16[2048,768]{1,0:T(8,128)(2,1)}), bf16[512,768]{1,0:T(8,128)(2,1)}) %reduce-scatter.15.cloned.1.call-update) | async-done | bytes 786448 | tf_op jit(solution)/shard_map/reduce_scatter | solution.py:211
  408.2 3.1 multiply_reduce_fusion.1
  416.9 28.4 %all-gather.17.cloned.1.call-done = bf16[2048,768]{1,0:T(8,128)(2,1)} async-done(((bf16[512,768]{1,0:T(8,128)(2,1)}), bf16[2048,768]{1,0:T(8,128)(2,1)}) %all-gather.17.cloned.1.call-update) | async-done | bytes 3145744 | tf_op jit(solution)/shard_map/all_gather | solution.py:217
  445.3 3.1 convolution_convert_fusion.3
  450.1 57.5 %while.56 = (s32[]{:T(128)}, bf16[2,1024,3,64]{3,2,1,0:T(4,128)(2,1)}, bf16[2,1024,3,64]{1,3,2,0:T(8,128)(2,1)}, bf16[2,1024,3,64]{1,3,2,0:T(8,128)(2,1)}, bf16[...) while((s32[]{:T(128)}, ...), condition=%wide.region_21.22_spmd, body=%wide.region_17.21_spmd.sunk | while | flops 1031798272 | bytes 74459688 | solution.py:220
  455.9 18.2 %while.58 = (s32[]{:T(128)}, f32[1024,3,64]{0,2,1:T(8,128)S(1)}, f32[1024,3,64]{0,2,1:T(8,128)}, bf16[2,512,3,64]{1,3,2,0:T(8,128)(2,1)S(1)}, bf16[2,512,3,64]{1...) while((s32[]{:T(128)}, f32[1024,3,64]{0,2,1:T(8,128)S(1)}, ...), condition=%wide.region_20.20_spmd.clone, body=%wide.region_18.19_spmd.clone.sunk | while | flops 1031405056 | bytes 58837208 | solution.py:106
  459.3 2.1 multiply_reduce_fusion.6
  468.4 2.1 multiply_reduce_fusion.6
  484.6 18.2 %while.58 = (s32[]{:T(128)}, f32[1024,3,64]{0,2,1:T(8,128)S(1)}, f32[1024,3,64]{0,2,1:T(8,128)}, bf16[2,512,3,64]{1,3,2,0:T(8,128)(2,1)S(1)}, bf16[2,512,3,64]{1...) while((s32[]{:T(128)}, f32[1024,3,64]{0,2,1:T(8,128)S(1)}, ...), condition=%wide.region_20.20_spmd.clone, body=%wide.region_18.19_spmd.clone.sunk | while | flops 1031405056 | bytes 58837208 | solution.py:106
  488.1 2.1 multiply_reduce_fusion.6
  497.2 2.1 multiply_reduce_fusion.6
  507.6 4.5 convolution_bitcast_fusion
  512.4 3.6 copy.80
  516.0 2.6 stack_reshape.9
  523.8 2.5 stack_reshape.11
  528.2 6.1 bitcast_convert_fusion
  534.4 7.0 fusion.72
  541.7 7.0 fusion.73
  548.8 4.6 fusion.71
  553.4 2.0 copy.83
  556.1 3.8 convert_reduce_fusion.1
  560.4 40.9 %all-reduce = (f32[768]{0:T(1024)}, f32[768]{0:T(1024)}, f32[768]{0:T(1024)}, f32[768]{0:T(1024)}, f32[768]{0:T(1024)}, /*index=5*/f32[3072]{0:T(1024)}, f32[768]{0:T(1024)}, f32[768]{0:T(1024)}, f32[768]{0:T(1024)}) all-reduce(f32[768]{0:T(1024)S(1)} %dynamic_update_slice.38, ...), channel_id=1, replica_groups=mesh['dp'=8,'tensor'=4] {'dp','tensor'}, use_global_device_ids=true, to_apply=%region_25.26 | all-reduce | flops 9216 | bytes 73728 | tf_op jit(solution)/shard_map/psum | solution.py:256
  602.9 12.4 %reduce-scatter.17.cloned.1.call-done = bf16[512,768]{1,0:T(8,128)(2,1)} async-done(((bf16[2048,768]{1,0:T(8,128)(2,1)}), bf16[512,768]{1,0:T(8,128)(2,1)}) %reduce-scatter.17.cloned.1.call-update) | async-done | bytes 786448 | tf_op jit(solution)/shard_map/reduce_scatter | solution.py:243
  615.3 2.5 convert_add_fusion
  617.8 71.2 %reduce-scatter.21.cloned.1.call-done = f32[96,768]{1,0:T(8,128)} async-done(((f32[768,768]{1,0:T(8,128)}), f32[96,768]{1,0:T(8,128)}) %reduce-scatter.21.cloned.1.call-update) | async-done | bytes 294928 | tf_op jit(solution)/shard_map/reduce_scatter | solution.py:253
  689.0 73.2 %reduce-scatter.23.cloned.1.call-done = f32[768,96]{0,1:T(8,128)} async-done(((f32[768,768]{0,1:T(8,128)}), f32[768,96]{0,1:T(8,128)}) %reduce-scatter.23.cloned.1.call-update) | async-done | bytes 294928 | tf_op jit(solution)/shard_map/reduce_scatter | solution.py:254
  762.2 73.1 %reduce-scatter.19.cloned.1.call-done = f32[96,3,192]{2,0,1:T(8,128)} async-done(((f32[768,3,192]{2,0,1:T(8,128)}), f32[96,3,192]{2,0,1:T(8,128)}) %reduce-scatter.19.cloned.1.call-update) | async-done | bytes 221200 | tf_op jit(solution)/shard_map/reduce_scatter | solution.py:251
  (304 shorter events, 133.4 us)
Async XLA Ops:
  8.0 72.4 %all-gather.7.cloned.1.call-start = ((), (), s32[]{:S(2)}) async-start(), calls=%async_computation.8 | async-start | bytes 3932160 | tf_op jit(solution)/shard_map/all_gather | solution.py:157
  8.7 156.6 %reduce-scatter.11.cloned.1.call-start = ((), (), s32[]{:S(2)}) async-start(), calls=%async_computation.9 | async-start | bytes 3932160 | tf_op jit(solution)/shard_map/reduce_scatter | solution.py:170
  46.6 37.7 %copy-start.14 = (bf16[768,3,192]{2,0,1:T(8,128)(2,1)}, bf16[768,3,192]{2,0,1:T(8,128)(2,1)S(1)}, u32[]{:S(2)}) copy-start(bf16[768,3,192]{2,0,1:T(8,128)(2,1)S(1)} %all_gather.28) | copy-start | bytes 2654212
  88.7 35.1 %copy-start.17 = (bf16[192,768]{0,1:T(8,128)(2,1)S(1)}, bf16[192,768]{0,1:T(8,128)(2,1)}, u32[]{:S(2)}) copy-start(bf16[192,768]{0,1:T(8,128)(2,1)} %all_gather.29) | copy-start | bytes 884740
  123.8 41.6 %copy-start = (bf16[512,768]{1,0:T(8,128)(2,1)S(1)}, bf16[512,768]{1,0:T(8,128)(2,1)}, u32[]{:S(2)}) copy-start(bf16[512,768]{1,0:T(8,128)(2,1)} %param.24) | copy-start | bytes 2359300
  123.8 41.6 %copy-start.22 = (f32[768]{0:T(1024)S(1)}, f32[768]{0:T(1024)}, u32[]{:S(2)}) copy-start(f32[768]{0:T(1024)} %param.31) | copy-start | bytes 9220
  126.5 42.0 %copy-start.24 = (f32[768]{0:T(1024)S(1)}, f32[768]{0:T(1024)}, u32[]{:S(2)}) copy-start(f32[768]{0:T(1024)} %param.32) | copy-start | bytes 9220
  126.5 42.0 %copy-start.38 = (f32[768]{0:T(1024)S(1)}, f32[768]{0:T(1024)}, u32[]{:S(2)}) copy-start(f32[768]{0:T(1024)} %param.33) | copy-start | bytes 9220
  126.5 90.2 %all-gather.11.cloned.1.call-start = ((), (), s32[]{:S(2)}) async-start(), calls=%async_computation.11 | async-start | bytes 1327104 | tf_op jit(solution)/shard_map/all_gather | solution.py:150
  127.1 42.9 %copy-start.16 = (bf16[768,96]{0,1:T(8,128)(2,1)S(1)}, bf16[768,96]{0,1:T(8,128)(2,1)}, u32[]{:S(2)}) copy-start(bf16[768,96]{0,1:T(8,128)(2,1)} %param.36) | copy-start | bytes 442372
  127.1 89.6 %all-gather.9.cloned.1.call-start = ((), (), s32[]{:S(2)}) async-start(), calls=%async_computation.10 | async-start | bytes 3932160 | tf_op jit(solution)/shard_map/all_gather | solution.py:179
  168.5 8.7 %copy-start.30 = (f32[512]{0:T(512)}, f32[512]{0:T(512)S(1)}, u32[]{:S(2)}) copy-start(f32[512]{0:T(512)S(1)} %multiply_reduce_fusion.4) | copy-start | bytes 6148
  168.5 45.2 %copy-start.25 = (f32[512]{0:T(512)}, f32[512]{0:T(512)S(1)}, u32[]{:S(2)}) copy-start(f32[512]{0:T(512)S(1)} %fusion.63) | copy-start | bytes 6148
  169.9 111.4 %reduce-scatter.13.cloned.1.call-start = ((), (), s32[]{:S(2)}) async-start(), calls=%async_computation.12 | async-start | bytes 3932160 | tf_op jit(solution)/shard_map/reduce_scatter | solution.py:183
  170.0 7.2 collective-permute-start
  177.2 7.8 collective-permute-start.1
  185.9 27.1 %collective-permute-start.2 = (bf16[768,384]{0,1:T(8,128)(2,1)}, bf16[768,384]{0,1:T(8,128)(2,1)S(1)}, u32[]{:S(2)}, u32[]{:S(2)}) collective-permute-start(bf16[768,384]{0,1:T(8,128)(2,1)} %pad_maximum_fusion), channel_id=1, source_target_pairs={{0,16},{4,20},{8,24},{12,28},{16,0},{20,4},{24,8},{28,12},{1,17},{... | collective-permute-start | bytes 1769480 | tf_op jit(solution)/shard_map/ppermute | solution.py:19
  187.3 48.1 %copy-start.40 = (f32[768]{0:T(1024)}, f32[768]{0:T(1024)S(1)}, u32[]{:S(2)}) copy-start(f32[768]{0:T(1024)S(1)} %dynamic_slice.62) | copy-start | bytes 9220
  242.5 38.8 %copy-start.1 = (bf16[512,768]{1,0:T(8,128)(2,1)S(1)}, bf16[512,768]{1,0:T(8,128)(2,1)}, u32[]{:S(2)}) copy-start(bf16[512,768]{1,0:T(8,128)(2,1)} %add_convert_fusion.3) | copy-start | bytes 2359300
  242.5 38.8 %copy-start.23 = (f32[768]{0:T(1024)S(1)}, f32[768]{0:T(1024)}, u32[]{:S(2)}) copy-start(f32[768]{0:T(1024)} %param.37) | copy-start | bytes 9220
  242.5 42.0 %copy-start.21 = (bf16[512,768]{1,0:T(8,128)(2,1)S(1)}, bf16[512,768]{1,0:T(8,128)(2,1)}, u32[]{:S(2)}) copy-start(bf16[512,768]{1,0:T(8,128)(2,1)} %param.25) | copy-start | bytes 2359300
  242.5 82.4 %all-gather.15.cloned.1.call-start = ((), (), s32[]{:S(2)}) async-start(), calls=%async_computation.14 | async-start | bytes 1327104 | tf_op jit(solution)/shard_map/all_gather | solution.py:200
  243.2 110.0 %all-gather.13.cloned.1.call-start = ((), (), s32[]{:S(2)}) async-start(), calls=%async_computation.13 | async-start | bytes 3932160 | tf_op jit(solution)/shard_map/all_gather | solution.py:205
  281.3 4.6 copy-start.42
  287.6 65.7 %copy-start.41 = (f32[768]{0:T(1024)S(1)}, f32[768]{0:T(1024)}, u32[]{:S(2)}) copy-start(f32[768]{0:T(1024)} %copy-done.40) | copy-start | bytes 9220
  287.6 76.8 %copy-start.27 = (f32[512]{0:T(512)}, f32[512]{0:T(512)S(1)}, u32[]{:S(2)}) copy-start(f32[512]{0:T(512)S(1)} %negate_multiply_fusion.2) | copy-start | bytes 6148
  289.8 118.4 %reduce-scatter.15.cloned.1.call-start = ((), (), s32[]{:S(2)}) async-start(), calls=%async_computation.15 | async-start | bytes 3932160 | tf_op jit(solution)/shard_map/reduce_scatter | solution.py:211
  353.3 12.8 %copy-start.43 = (bf16[768,768]{1,0:T(8,128)(2,1)S(1)}, bf16[768,768]{1,0:T(8,128)(2,1)}, u32[]{:S(2)}) copy-start(bf16[768,768]{1,0:T(8,128)(2,1)} %all-gather.11.cloned.1.call-done) | copy-start | bytes 3538948
  370.1 38.1 %copy-start.3 = (f32[512,768]{1,0:T(8,128)S(1)}, f32[512,768]{1,0:T(8,128)}, u32[]{:S(2)}) copy-start(f32[512,768]{1,0:T(8,128)} %copy-done.2) | copy-start | bytes 4718596
  370.1 38.1 %copy-start.26 = (f32[512]{0:T(512)S(1)}, f32[512]{0:T(512)}, u32[]{:S(2)}) copy-start(f32[512]{0:T(512)} %copy-done.25) | copy-start | bytes 6148
  370.2 75.2 %all-gather.17.cloned.1.call-start = ((), (), s32[]{:S(2)}) async-start(), calls=%async_computation.16 | async-start | bytes 3932160 | tf_op jit(solution)/shard_map/all_gather | solution.py:217
  408.2 3.8 copy-start.18
  416.6 184.6 %reduce-scatter.25.cloned.1.call-start = ((), (), s32[]{:S(2)}) async-start(), calls=%async_computation.21 | async-start | bytes 884736
  507.6 4.8 copy-start.13
  512.2 103.1 %reduce-scatter.17.cloned.1.call-start = ((), (), s32[]{:S(2)}) async-start(), calls=%async_computation.17 | async-start | bytes 3932160 | tf_op jit(solution)/shard_map/reduce_scatter | solution.py:243
  516.0 6.2 copy-start.19
  522.2 6.1 copy-start.15
  534.3 154.6 %reduce-scatter.21.cloned.1.call-start = ((), (), s32[]{:S(2)}) async-start(), calls=%async_computation.19 | async-start | bytes 2654208 | tf_op jit(solution)/shard_map/reduce_scatter | solution.py:253
  541.4 220.7 %reduce-scatter.23.cloned.1.call-start = ((), (), s32[]{:S(2)}) async-start(), calls=%async_computation.20 | async-start | bytes 2654208 | tf_op jit(solution)/shard_map/reduce_scatter | solution.py:254
  548.7 286.5 %reduce-scatter.19.cloned.1.call-start = ((), (), s32[]{:S(2)}) async-start(), calls=%async_computation.18 | async-start | bytes 2654208 | tf_op jit(solution)/shard_map/reduce_scatter | solution.py:251
  555.4 4.9 copy-start.31
  555.4 4.9 copy-start.32
  555.4 4.9 copy-start.33
  555.4 4.9 copy-start.34
  555.4 4.9 copy-start.35
  555.4 4.9 copy-start.36
  555.5 59.8 %copy-start.10 = (f32[512,768]{1,0:T(8,128)S(1)}, f32[512,768]{1,0:T(8,128)}, u32[]{:S(2)}) copy-start(f32[512,768]{1,0:T(8,128)} %copy-done.9) | copy-start | bytes 4718596
  555.5 59.8 %copy-start.29 = (f32[512]{0:T(512)S(1)}, f32[512]{0:T(512)}, u32[]{:S(2)}) copy-start(f32[512]{0:T(512)} %copy-done.28) | copy-start | bytes 6148
  (23 other events, 48.7 us)
Sparse Core Ops, SparseCore 0:
  10.4 31.2 all-gather.6
  126.7 38.6 reduce-scatter.10
  370.3 37.8 reduce-scatter.14
  416.8 28.5 all-gather.16
Sparse Core Ops, SparseCore 1:
  129.2 42.2 all-gather.10
  173.4 26.7 all-gather.8
  242.6 38.6 reduce-scatter.12
  283.5 41.4 all-gather.14
  326.5 26.7 all-gather.12
  512.3 63.2 reduce-scatter.24
  578.0 37.3 reduce-scatter.16
  619.2 69.7 reduce-scatter.20
  692.9 69.2 reduce-scatter.22
  766.3 69.0 reduce-scatter.18
